TPU v7x, 32 devices: a whole 2x2x4 slice. The times are simulated.
32 devices in a mesh: dp: 8 (over y, x, core), tensor: 4 (over z).
Axes of the slice: x: 2, y: 2, z: 4, core: 2. Of those that a mesh axis runs over, the one named last changes fastest.
Arguments:
- tokens: bfloat16 [6400, 1024], P('dp'), may hold values from -10.5 to 10.5, as said below
- blank_mask: int32 [64], P('dp'), may hold values 0 or 1
- norm_gain: float32 [2, 1024], replicated, may hold values from 0.25 to 1.75
- norm_bias: float32 [2, 1024], replicated, may hold values from -1.8 to 1.8
- w_qkv: bfloat16 [3, 1024, 1024], P(None, None, 'tensor'), may hold values from -0.1875 to 0.1875
- qv_bias: float32 [2, 1024], P(None, 'tensor'), may hold values from -1.8 to 1.8
- rel_bias: float32 [32, 361], P('tensor'), may hold values from -5 to 5
- w_out: bfloat16 [1024, 1024], P('tensor'), may hold values from -0.75 to 0.75
- out_bias: float32 [2, 1024], replicated, may hold values from -1.8 to 1.8
- w_up: bfloat16 [1024, 4096], P(None, 'tensor'), may hold values from -0.1875 to 0.1875
- up_bias: float32 [4096], P('tensor'), may hold values from -1.8 to 1.8
- w_down: bfloat16 [4096, 1024], P('tensor'), may hold values from -0.09375 to 0.09375
- grad_out: bfloat16 [6400, 1024], P('dp'), may hold values from -6 to 6
Outputs:
- output: bfloat16 [6400, 1024], P(('dp', 'tensor'))
- grad_tokens: float32 [6400, 1024], P(('dp', 'tensor'))
- grad_norm_gain: float32 [2, 1024], replicated
- grad_norm_bias: float32 [2, 1024], replicated
- grad_w_qkv: float32 [3, 1024, 1024], P(None, None, 'tensor')
- grad_qv_bias: float32 [2, 1024], P(None, 'tensor')
- grad_rel_bias: float32 [32, 361], P('tensor')
- grad_w_out: float32 [1024, 1024], P('tensor')
- grad_out_bias: float32 [2, 1024], replicated
- grad_w_up: float32 [1024, 4096], P(None, 'tensor')
- grad_up_bias: float32 [4096], P('tensor')
- grad_w_down: float32 [4096, 1024], P('tensor')
- root_means: float32 [3], replicated
Inputs may be any that keep to these rules, and one draw needn't show every extreme that they name: `tokens`: values are of order one, with row scales differing between windows. `blank_mask`: 1 marks a blank window.
All inputs are finite; a program needn't handle non-finite values. No bound on the sum of `blank_mask` on one device may be relied on, other than what follows from the above.
Results may differ from a plain program's by a relative error of at most 0.0095.
The roundings to bfloat16 on the way count: a program that leaves them out, or rounds other values in their place, can miss the bound.
Values may be sent and summed in bfloat16 or wider, within the bound.
A program may use at most 128 MiB of HBM per device.

v0:
```python
import jax
import jax.numpy as jnp
from jax import lax
from jax.sharding import PartitionSpec as P

WS = 10


highest = lax.Precision.HIGHEST
norm_eps = 1e-05
half_root = 0.7071067811865476
gauss_norm = 0.3989422804014327


def normalize(values):
    center = jnp.mean(values, axis=-1, keepdims=True)
    shifted = values - center
    spread = jnp.mean(shifted * shifted, axis=-1, keepdims=True)
    inverse = lax.rsqrt(spread + norm_eps)
    return (shifted * inverse, inverse)


def norm_back(gradient, normed_hat, inverse, gain_row):
    scaled = gradient * gain_row
    inner_sum = jnp.mean(scaled, axis=-1, keepdims=True)
    cross_sum = jnp.mean(scaled * normed_hat, axis=-1, keepdims=True)
    return inverse * (scaled - inner_sum - normed_hat * cross_sum)


def relative_onehot(window_side):
    positions = jnp.arange(window_side)
    offset_grid = positions[:, None] - positions[None, :] + (window_side - 1)
    return (offset_grid[:, :, None] == jnp.arange(2 * window_side - 1)[None, None, :]).astype(
        jnp.float32
    )


def relative(bias_table, window_side):
    onehot = relative_onehot(window_side)
    heads_count = bias_table.shape[0]
    square = bias_table.reshape(heads_count, 2 * window_side - 1, 2 * window_side - 1)
    spread_full = jnp.einsum("ija,klb,hab->hikjl", onehot, onehot, square, precision=highest)
    return spread_full.reshape(heads_count, window_side * window_side, window_side * window_side)


def relative_back(gradient, window_side):
    onehot = relative_onehot(window_side)
    heads_count = gradient.shape[0]
    grad_grid = gradient.reshape(heads_count, window_side, window_side, window_side, window_side)
    folded = jnp.einsum("hikjl,ija,klb->hab", grad_grid, onehot, onehot, precision=highest)
    return folded.reshape(heads_count, (2 * window_side - 1) ** 2)


def on_device(
    tokens,
    blank_mask,
    norm_gain,
    norm_bias,
    w_qkv,
    qv_bias,
    rel_bias,
    w_out,
    out_bias,
    w_up,
    up_bias,
    w_down,
    grad_out,
):
    tensor_count = lax.axis_size("tensor")
    rows_all = tokens.shape[0]
    rows_own = rows_all // tensor_count
    row_start = lax.axis_index("tensor") * rows_own
    window_area = WS * WS
    windows = rows_all // window_area
    heads_here = rel_bias.shape[0]
    width_here = w_out.shape[0]
    head_dim = width_here // heads_here
    score_scale = head_dim ** (-0.5)

    def own_rows(values):
        return lax.dynamic_slice_in_dim(values, row_start, rows_own, 0)

    source = tokens.astype(jnp.float32)
    hat_one, inv_one = normalize(source)
    normed_one = (hat_one * norm_gain[0] + norm_bias[0]).astype(jnp.bfloat16)
    projected = jnp.einsum("rd,tde->tre", normed_one, w_qkv, preferred_element_type=jnp.float32)
    shifts = jnp.stack([qv_bias[0], jnp.zeros_like(qv_bias[0]), qv_bias[1]])
    projected = (projected + shifts[:, None, :]).astype(jnp.bfloat16)
    projected = projected.reshape(3, windows, window_area, heads_here, head_dim)
    query_part, key_part, value_part = (projected[0], projected[1], projected[2])
    bias_block = relative(rel_bias, WS)

    def scores_of():
        raw_scores = jnp.einsum(
            "wihc,wjhc->whij", query_part, key_part, preferred_element_type=jnp.float32
        )
        return raw_scores * score_scale + bias_block[None]

    scores = scores_of()
    row_top = jnp.max(scores, axis=-1, keepdims=True)
    exponent = jnp.exp(scores - row_top)
    row_total = jnp.sum(exponent, axis=-1, keepdims=True)
    log_total = row_top + jnp.log(row_total)
    weights = (exponent / row_total).astype(jnp.bfloat16)
    mixed_heads = jnp.einsum(
        "whij,wjhc->wihc", weights, value_part, preferred_element_type=jnp.float32
    )
    mixed_heads = mixed_heads.astype(jnp.bfloat16).reshape(rows_all, width_here)
    attn_part = jnp.dot(mixed_heads, w_out, preferred_element_type=jnp.float32)
    alive_rows = jnp.repeat(1.0 - blank_mask.astype(jnp.float32), window_area)
    alive_own = own_rows(alive_rows)[:, None]
    source_own = own_rows(source)
    attn_own = lax.psum_scatter(attn_part, "tensor", scatter_dimension=0, tiled=True) + out_bias[0]
    resid_own = source_own + attn_own
    hat_two, inv_two = normalize(resid_own)
    normed_rows = (hat_two * norm_gain[1] + norm_bias[1]).astype(jnp.bfloat16)
    normed_two = lax.all_gather(normed_rows, "tensor", axis=0, tiled=True)
    hidden = jnp.dot(normed_two, w_up, preferred_element_type=jnp.float32) + up_bias
    active = jax.nn.gelu(hidden, approximate=False).astype(jnp.bfloat16)
    mlp_part = jnp.dot(active, w_down, preferred_element_type=jnp.float32)
    branch_own = lax.psum_scatter(mlp_part, "tensor", scatter_dimension=0, tiled=True) + out_bias[1]
    output = (resid_own + branch_own).astype(jnp.bfloat16)
    stat_terms = jnp.stack(
        [
            jnp.sum(alive_own * source_own * source_own),
            jnp.sum(alive_own * attn_own * attn_own),
            jnp.sum(alive_own * branch_own * branch_own),
            jnp.sum(alive_own),
        ]
    )
    stat_total = lax.psum(stat_terms, ("dp", "tensor"))
    grad_full = grad_out.astype(jnp.float32)
    grad_down = jnp.einsum("rf,rd->fd", active, grad_out, preferred_element_type=jnp.float32)
    grad_active = jnp.einsum("rd,fd->rf", grad_out, w_down, preferred_element_type=jnp.float32)
    gelu_slope = (
        0.5 * (1.0 + lax.erf(hidden * half_root))
        + hidden * jnp.exp(-0.5 * hidden * hidden) * gauss_norm
    )
    grad_hidden = (grad_active * gelu_slope).astype(jnp.bfloat16)
    grad_up_bias = jnp.sum(grad_hidden.astype(jnp.float32), axis=0)
    grad_up = jnp.einsum("rd,rf->df", normed_two, grad_hidden, preferred_element_type=jnp.float32)
    norm_part = jnp.einsum("rf,df->rd", grad_hidden, w_up, preferred_element_type=jnp.float32)
    grad_norm_own = lax.psum_scatter(norm_part, "tensor", scatter_dimension=0, tiled=True)
    grad_resid_own = own_rows(grad_full) + norm_back(grad_norm_own, hat_two, inv_two, norm_gain[1])
    grad_attn = lax.all_gather(grad_resid_own.astype(jnp.bfloat16), "tensor", axis=0, tiled=True)
    gain_two = jnp.sum(grad_norm_own * hat_two, axis=0)
    shift_two = jnp.sum(grad_norm_own, axis=0)
    attn_bias_term = jnp.sum(own_rows(grad_attn).astype(jnp.float32), axis=0)
    mlp_bias_term = jnp.sum(own_rows(grad_full), axis=0)
    grad_wout = jnp.einsum("re,rd->ed", mixed_heads, grad_attn, preferred_element_type=jnp.float32)
    grad_mixed = jnp.einsum("rd,ed->re", grad_attn, w_out, preferred_element_type=jnp.float32)
    grad_mixed = grad_mixed.astype(jnp.bfloat16).reshape(windows, window_area, heads_here, head_dim)
    probs_full = jnp.exp(scores_of() - log_total)
    probs_low = probs_full.astype(jnp.bfloat16)
    grad_values = jnp.einsum(
        "whij,wihc->wjhc", probs_low, grad_mixed, preferred_element_type=jnp.float32
    )
    grad_probs = jnp.einsum(
        "wihc,wjhc->whij", grad_mixed, value_part, preferred_element_type=jnp.float32
    )
    inner_sum = jnp.sum(grad_probs * probs_full, axis=-1, keepdims=True)
    grad_scores = (probs_full * (grad_probs - inner_sum)).astype(jnp.bfloat16)
    grad_table = relative_back(jnp.sum(grad_scores.astype(jnp.float32), axis=0), WS)
    grad_query = (
        jnp.einsum("whij,wjhc->wihc", grad_scores, key_part, preferred_element_type=jnp.float32)
        * score_scale
    )
    grad_keys = (
        jnp.einsum("whij,wihc->wjhc", grad_scores, query_part, preferred_element_type=jnp.float32)
        * score_scale
    )
    grad_proj = (
        jnp.stack([grad_query, grad_keys, grad_values])
        .astype(jnp.bfloat16)
        .reshape(3, rows_all, width_here)
    )
    grad_qv = jnp.stack(
        [
            jnp.sum(grad_proj[0].astype(jnp.float32), axis=0),
            jnp.sum(grad_proj[2].astype(jnp.float32), axis=0),
        ]
    )
    grad_qkv = jnp.einsum("rd,tre->tde", normed_one, grad_proj, preferred_element_type=jnp.float32)
    input_part = jnp.einsum("tre,tde->rd", grad_proj, w_qkv, preferred_element_type=jnp.float32)
    grad_in_own = lax.psum_scatter(input_part, "tensor", scatter_dimension=0, tiled=True)
    hat_one_own = own_rows(hat_one)
    grad_tokens = grad_resid_own + norm_back(
        grad_in_own, hat_one_own, own_rows(inv_one), norm_gain[0]
    )
    gain_one = jnp.sum(grad_in_own * hat_one_own, axis=0)
    shift_one = jnp.sum(grad_in_own, axis=0)
    gain_terms = jnp.stack([gain_one, gain_two])
    shift_terms = jnp.stack([shift_one, shift_two])
    bias_terms = jnp.stack([attn_bias_term, mlp_bias_term])
    gain_sums, shift_sums, bias_sums = lax.psum(
        (gain_terms, shift_terms, bias_terms), ("dp", "tensor")
    )
    grad_qkv, grad_qv, grad_table, grad_wout, grad_up, grad_up_bias, grad_down = lax.psum(
        (grad_qkv, grad_qv, grad_table, grad_wout, grad_up, grad_up_bias, grad_down), "dp"
    )
    live_count = jnp.maximum(stat_total[3], 1.0) * tokens.shape[1]
    root_means = jnp.sqrt(stat_total[0:3] / live_count)
    return (
        output,
        grad_tokens,
        gain_sums,
        shift_sums,
        grad_qkv,
        grad_qv,
        grad_table,
        grad_wout,
        bias_sums,
        grad_up,
        grad_up_bias,
        grad_down,
        root_means,
    )


def solution(mesh):
    in_specs = (
        P("dp", None),
        P("dp"),
        P(),
        P(),
        P(None, None, "tensor"),
        P(None, "tensor"),
        P("tensor", None),
        P("tensor", None),
        P(),
        P(None, "tensor"),
        P("tensor"),
        P("tensor", None),
        P("dp", None),
    )
    out_specs = (
        P(("dp", "tensor"), None),
        P(("dp", "tensor"), None),
        P(),
        P(),
        P(None, None, "tensor"),
        P(None, "tensor"),
        P("tensor", None),
        P("tensor", None),
        P(),
        P(None, "tensor"),
        P("tensor"),
        P("tensor", None),
        P(),
    )
    return jax.shard_map(
        on_device, mesh=mesh, in_specs=in_specs, out_specs=out_specs, check_vma=False
    )
```

profile of v0, /device:TPU:0, one launch (start us, length us, event | category | flops | bytes accessed | tf_op | source)
XLA Modules:
  0.0 663.5 jit_solution(12015706099472850518)
XLA Ops:
  8.7 4.8 convolution_bitcast_fusion
  13.5 4.4 reshape.173
  32.4 2.4 squeeze.12
  39.6 3.5 fusion.72
  43.4 3.5 convert_element_type.72
  47.0 61.5 %reduce-scatter.5.cloned.1.call-done = f32[200,1024]{1,0:T(8,128)} async-done(((f32[800,1024]{1,0:T(8,128)}), f32[200,1024]{1,0:T(8,128)}) %reduce-scatter.5.cloned.1.call-update) | async-done | bytes 819216 | tf_op jit(solution)/shard_map/reduce_scatter | solution.py:113
  111.3 38.2 %all-gather.3.cloned.1.call-done = bf16[800,1024]{1,0:T(8,128)(2,1)} async-done(((bf16[200,1024]{1,0:T(8,128)(2,1)}), bf16[800,1024]{1,0:T(8,128)(2,1)}) %all-gather.3.cloned.1.call-update) | async-done | bytes 1638416 | tf_op jit(solution)/shard_map/all_gather | solution.py:117
  149.5 10.8 %fusion.2 = (bf16[800,1024]{1,0:T(8,128)(2,1)}, f32[800,1024]{1,0:T(8,128)S(1)}) fusion(f32[1024]{0:T(1024)S(1)} %copy-done.49, bf16[800,1024]{1,0:T(8,128)(2,1)} %all-gather.3.cloned.1.call-done, bf16[1024,1024]{1,0:T(8,128)(2,1)S(1)} %copy-done), kind=kOutput, calls=%fused_computation.11 | convolution fusion | flops 1731788800 | bytes 8654848 | tf_op jit(solution)/shard_map/dot_general | solution.py:118
  160.4 3.7 convert_reduce_fusion.1
  165.3 3.6 fusion.74
  170.5 5.0 fusion.73
  177.0 53.4 %reduce-scatter.9.cloned.1.call-done = f32[200,1024]{1,0:T(8,128)} async-done(((f32[800,1024]{1,0:T(8,128)}), f32[200,1024]{1,0:T(8,128)}) %reduce-scatter.9.cloned.1.call-update) | async-done | bytes 819216 | tf_op jit(solution)/shard_map/reduce_scatter | solution.py:143
  232.6 63.0 %reduce-scatter.7.cloned.1.call-done = f32[200,1024]{1,0:T(8,128)} async-done(((f32[800,1024]{1,0:T(8,128)}), f32[200,1024]{1,0:T(8,128)}) %reduce-scatter.7.cloned.1.call-update) | async-done | bytes 819216 | tf_op jit(solution)/shard_map/reduce_scatter | solution.py:121
  295.6 4.1 fusion.36
  300.2 6.5 fusion.77
  306.7 4.4 fusion.76
  311.1 26.9 %all-gather.5.cloned.1.call-done = bf16[800,1024]{1,0:T(8,128)(2,1)} async-done(((bf16[200,1024]{1,0:T(8,128)(2,1)}), bf16[800,1024]{1,0:T(8,128)(2,1)}) %all-gather.5.cloned.1.call-update) | async-done | bytes 1638416 | tf_op jit(solution)/shard_map/all_gather | solution.py:145
  338.0 2.9 convolution_convert_fusion
  342.9 2.4 reshape.158
  345.3 2.8 convert_reduce_fusion.3
  358.2 4.9 convolution_bitcast_fusion.2
  365.8 4.8 convolution_bitcast_fusion.1
  373.5 2.7 pad_maximum_fusion.8
  376.4 4.0 reshape.174
  380.3 12.3 %copy.101 = f32[8,10,10,10,10]{4,3,1,2,0:T(8,128)} copy(f32[8,10,10,10,10]{2,1,4,3,0:T(8,128)} %reshape.174) | data formatting | bytes 640000 | tf_op jit(solution)/shard_map/reshape | solution.py:49
  392.6 8.5 %convolution_bitcast_fusion.3 = f32[19,8,10,10]{0,3,2,1:T(8,128)S(1)} fusion(f32[8,10,10,10,10]{4,3,1,2,0:T(8,128)} %copy.101, s32[10,10]{1,0:T(8,128)S(1)} %copy-done.24), kind=kOutput, calls=%fused_computation.55 | convolution fusion | flops 18241900 | bytes 381200 | tf_op jit(solution)/shard_map/hikjl,ija,klb->hab/dot_general | solution.py:50
  402.0 25.5 %all-reduce.1 = (f32[2,256]{1,0:T(2,128)}, f32[8,361]{1,0:T(8,128)}, f32[1024]{0:T(1024)}) all-reduce(f32[2,256]{1,0:T(2,128)S(1)} %pad_maximum_fusion.7, f32[8,361]{1,0:T(8,128)S(1)} %reshape.160, f32[1024]{0:T(1024)S(1)} %copy-done.43), channel_id=1, replica_groups=mesh['dp'=8,'tensor'=4] {'dp'}, use_global_device_ids=true, to_apply=%region_24.0 | all-reduce | flops 4424 | bytes 35392 | tf_op jit(solution)/shard_map/psum | solution.py:198
  427.4 109.0 %all-reduce.5.cloned.1.call-done = (f32[3,1024,256]{1,2,0:T(8,128)}, f32[256,1024]{1,0:T(8,128)}, f32[1024,1024]{1,0:T(8,128)}, f32[1024,1024]{1,0:T(8,128)}) async-done(((f32[3,1024,256]{1,2,0:T(8,128)}, f32[256,1024]{1,0:T(8,128)}, f32[1024,1024]{1,0:T(8,128)}, f32[1024,1024]{1,0:T(8,128)}), (f32[3,1024,256]{1,2,0:T(8,128)}, f32[256,1024]{1,0:T(8,128)}, f32[1024,1024]{1,0:T(8,128)}, ...) | async-done | bytes 12582928 | tf_op jit(solution)/shard_map/psum | solution.py:198
  536.4 3.6 copy.93
  540.0 61.3 %reduce-scatter.11.cloned.1.call-done = f32[200,1024]{1,0:T(8,128)} async-done(((f32[800,1024]{1,0:T(8,128)}), f32[200,1024]{1,0:T(8,128)}) %reduce-scatter.11.cloned.1.call-update) | async-done | bytes 819216 | tf_op jit(solution)/shard_map/reduce_scatter | solution.py:185
  603.0 40.8 %all-reduce = (f32[2,1024]{1,0:T(2,128)}, f32[2,1024]{1,0:T(2,128)}, f32[2,1024]{1,0:T(2,128)}, f32[4]{0:T(128)S(1)}) all-reduce(f32[2,1024]{1,0:T(2,128)S(1)} %pad_maximum_fusion.3, f32[2,1024]{1,0:T(2,128)S(1)} %pad_maximum_fusion.4, f32[2,1024]{1,0:T(2,128)S(1)} %pad_maximum_fusion.5, ...), channel_id=1, replica_groups=mesh['dp'=8,'tensor'=4] {'dp','tensor'}, use_global_device_ids=true, to_apply=%region_17.0 | all-reduce | flops 6148 | bytes 49184 | tf_op jit(solution)/shard_map/psum | solution.py:195
  645.9 2.5 multiply_add_fusion.1
  (192 shorter events, 59.8 us)
Async XLA Ops:
  7.2 142.3 %copy-start = (bf16[1024,1024]{1,0:T(8,128)(2,1)S(1)}, bf16[1024,1024]{1,0:T(8,128)(2,1)}, u32[]{:S(2)}) copy-start(bf16[1024,1024]{1,0:T(8,128)(2,1)} %param.22) | copy-start | bytes 6291460
  7.2 101.3 %reduce-scatter.5.cloned.1.call-start = ((), (), s32[]{:S(2)}) async-start(), calls=%async_computation.4 | async-start | bytes 4096000 | tf_op jit(solution)/shard_map/reduce_scatter | solution.py:113
  13.5 5.4 copy-start.44
  13.5 5.4 copy-start.39
  13.5 6.0 copy-start.40
  20.1 5.7 copy-start.29
  27.6 9.5 %copy-start.9 = (bf16[8,100,8,32]{1,0,3,2:T(8,128)(2,1)}, bf16[8,100,8,32]{1,0,3,2:T(8,128)(2,1)S(1)}, u32[]{:S(2)}) copy-start(bf16[8,100,8,32]{1,0,3,2:T(8,128)(2,1)S(1)} %squeeze.14) | copy-start | bytes 1228804
  31.4 5.6 copy-start.11
  43.1 67.1 %copy-start.26 = (f32[1,1024]{1,0:T(1,128)S(1)}, f32[1,1024]{1,0:T(1,128)}, u32[]{:S(2)}) copy-start(f32[1,1024]{1,0:T(1,128)} %get-tuple-element.92) | copy-start | bytes 12292
  43.1 67.1 %copy-start.37 = (f32[1,1024]{1,0:T(1,128)S(1)}, f32[1,1024]{1,0:T(1,128)}, u32[]{:S(2)}) copy-start(f32[1,1024]{1,0:T(1,128)} %get-tuple-element.94) | copy-start | bytes 12292
  43.2 106.4 %all-gather.3.cloned.1.call-start = ((), (), s32[]{:S(2)}) async-start(), calls=%async_computation.5 | async-start | bytes 2048000 | tf_op jit(solution)/shard_map/all_gather | solution.py:117
  46.9 102.6 %copy-start.49 = (f32[1024]{0:T(1024)S(1)}, f32[1024]{0:T(1024)}, u32[]{:S(2)}) copy-start(f32[1024]{0:T(1024)} %param.23) | copy-start | bytes 12292
  111.3 119.1 %reduce-scatter.9.cloned.1.call-start = ((), (), s32[]{:S(2)}) async-start(), calls=%async_computation.7 | async-start | bytes 4096000 | tf_op jit(solution)/shard_map/reduce_scatter | solution.py:143
  149.5 10.8 %copy-start.25 = (bf16[800,1024]{1,0:T(8,128)(2,1)S(1)}, bf16[800,1024]{1,0:T(8,128)(2,1)}, u32[]{:S(2)}) copy-start(bf16[800,1024]{1,0:T(8,128)(2,1)} %param.25) | copy-start | bytes 4915204
  149.5 10.8 %copy-start.45 = (bf16[1024,1024]{1,0:T(8,128)(2,1)S(1)}, bf16[1024,1024]{1,0:T(8,128)(2,1)}, u32[]{:S(2)}) copy-start(bf16[1024,1024]{1,0:T(8,128)(2,1)} %param.24) | copy-start | bytes 6291460
  169.0 126.7 %reduce-scatter.7.cloned.1.call-start = ((), (), s32[]{:S(2)}) async-start(), calls=%async_computation.6 | async-start | bytes 4096000 | tf_op jit(solution)/shard_map/reduce_scatter | solution.py:121
  175.5 120.1 %copy-start.16 = (f32[200,1024]{1,0:T(8,128)S(1)}, f32[200,1024]{1,0:T(8,128)}, u32[]{:S(2)}) copy-start(f32[200,1024]{1,0:T(8,128)} %reduce-scatter.5.cloned.1.call-done) | copy-start | bytes 2457604
  175.6 162.4 %all-gather.5.cloned.1.call-start = ((), (), s32[]{:S(2)}) async-start(), calls=%async_computation.8 | async-start | bytes 2048000 | tf_op jit(solution)/shard_map/all_gather | solution.py:145
  299.7 236.7 %all-reduce.5.cloned.1.call-start = ((), (), s32[]{:S(2)}) async-start(), calls=%async_computation.10 | async-start | bytes 25165824 | tf_op jit(solution)/shard_map/psum | solution.py:198
  300.2 6.5 copy-start.47
  300.2 6.5 copy-start.52
  311.1 34.2 %copy-start.3 = (f32[8,8,100,100]{2,3,1,0:T(8,128)S(1)}, f32[8,8,100,100]{2,3,1,0:T(8,128)}, u32[]{:S(2)}) copy-start(f32[8,8,100,100]{2,3,1,0:T(8,128)} %copy-done.2) | copy-start | bytes 7680004
  364.8 236.5 %reduce-scatter.11.cloned.1.call-start = ((), (), s32[]{:S(2)}) async-start(), calls=%async_computation.9 | async-start | bytes 4096000 | tf_op jit(solution)/shard_map/reduce_scatter | solution.py:185
  380.3 12.3 %copy-start.24 = (s32[10,10]{1,0:T(8,128)S(1)}, s32[10,10]{1,0:T(8,128)}, u32[]{:S(2)}) copy-start(s32[10,10]{1,0:T(8,128)} %copy-done.23) | copy-start | bytes 1204
  392.6 9.4 %copy-start.43 = (f32[1024]{0:T(1024)S(1)}, f32[1024]{0:T(1024)}, u32[]{:S(2)}) copy-start(f32[1024]{0:T(1024)} %get-tuple-element.108) | copy-start | bytes 12292
  401.8 199.5 %copy-start.6 = (f32[800,1024]{1,0:T(8,128)S(1)}, f32[800,1024]{1,0:T(8,128)}, u32[]{:S(2)}) copy-start(f32[800,1024]{1,0:T(8,128)} %subtract_multiply_fusion) | copy-start | bytes 9830404
  401.8 199.5 %copy-start.30 = (f32[1,1024]{1,0:T(1,128)S(1)}, f32[1,1024]{1,0:T(1,128)}, u32[]{:S(2)}) copy-start(f32[1,1024]{1,0:T(1,128)} %copy-done.29) | copy-start | bytes 12292
  536.4 66.5 %copy-start.36 = (f32[1024]{0:T(1024)S(1)}, f32[1024]{0:T(1024)}, u32[]{:S(2)}) copy-start(f32[1024]{0:T(1024)} %get-tuple-element.54) | copy-start | bytes 12292
  536.4 66.5 %copy-start.35 = (f32[1024]{0:T(1024)S(1)}, f32[1024]{0:T(1024)}, u32[]{:S(2)}) copy-start(f32[1024]{0:T(1024)} %get-tuple-element.59) | copy-start | bytes 12292
  536.4 66.6 %copy-start.38 = (f32[1024]{0:T(1024)S(1)}, f32[1024]{0:T(1024)}, u32[]{:S(2)}) copy-start(f32[1024]{0:T(1024)} %get-tuple-element.87) | copy-start | bytes 12292
  643.9 6.9 %copy-start.15 = (f32[1024,1024]{1,0:T(8,128)S(1)}, f32[1024,1024]{1,0:T(8,128)}, u32[]{:S(2)}) copy-start(f32[1024,1024]{1,0:T(8,128)} %get-tuple-element.120) | copy-start | bytes 12582916
  650.7 5.7 copy-start.1
  (28 other events, 85.7 us)
Sparse Core Ops, SparseCore 0:
  43.2 65.1 reduce-scatter.4
  111.4 38.0 all-gather.2
  169.1 61.2 reduce-scatter.8
  233.2 62.4 reduce-scatter.6
  299.8 38.0 all-gather.4
  364.9 171.4 all-reduce.4
  538.7 62.5 reduce-scatter.10
where the time goes:
time: 673 us; the launch traced here: 663 us
  waiting for transfers between devices  413 us (61%)
  matrix products  77.3 us (11%)
  blocking collectives  66.3 us (10%)
  local copies, waits for them, and re-layouts  60.4 us (9%)
  other arithmetic  29.4 us (4%)
  between operations  15.8 us (2%)
    psum x1, waiting for transfers between devices, on_device(): lax.psum((grad_qkv, grad_qv, grad_table, grad_wout, grad_up, grad_up_bias...  109 us
    reduce_scatter x1, waiting for transfers between devices, on_device(): lax.psum_scatter(mlp_part, 'tensor', scatter_dimension=0, tiled=True)  63 us
    reduce_scatter x1, waiting for transfers between devices, on_device(): lax.psum_scatter(attn_part, 'tensor', scatter_dimension=0, tiled=True)  61.5 us
    reduce_scatter x1, waiting for transfers between devices, on_device(): lax.psum_scatter(input_part, 'tensor', scatter_dimension=0, tiled=True)  61.3 us
    reduce_scatter x1, waiting for transfers between devices, on_device(): lax.psum_scatter(norm_part, 'tensor', scatter_dimension=0, tiled=True)  53.4 us
    psum x1, blocking collectives, on_device(): lax.psum((gain_terms, shift_terms, bias_terms), ('dp', 'tensor'))  40.8 us
    all_gather x1, waiting for transfers between devices, on_device(): normed_two = lax.all_gather(normed_rows, 'tensor', axis=0, tiled=True)  38.2 us
    all_gather x1, waiting for transfers between devices, on_device(): lax.all_gather(grad_resid_own.astype(jnp.bfloat16), 'tensor', axis=0, til...  26.9 us
  transfers between devices with their start and end apart: 7, of which 7 were waited for; matrix products, arithmetic and copies ran while one was open for 9% of the time, Pallas kernels for 0%

commit v1 on v0

--- a/solution.py
+++ b/solution.py
@@ -49,6 +49,13 @@
     grad_grid = gradient.reshape(heads_count, window_side, window_side, window_side, window_side)
     folded = jnp.einsum("hikjl,ija,klb->hab", grad_grid, onehot, onehot, precision=highest)
     return folded.reshape(heads_count, (2 * window_side - 1) ** 2)
+
+
+def scatter_rows(part):
+    sums = lax.psum_scatter(
+        part.astype(jnp.bfloat16), "tensor", scatter_dimension=0, tiled=True
+    )
+    return sums.astype(jnp.float32)
 
 
 def on_device(
@@ -110,7 +117,7 @@
     alive_rows = jnp.repeat(1.0 - blank_mask.astype(jnp.float32), window_area)
     alive_own = own_rows(alive_rows)[:, None]
     source_own = own_rows(source)
-    attn_own = lax.psum_scatter(attn_part, "tensor", scatter_dimension=0, tiled=True) + out_bias[0]
+    attn_own = scatter_rows(attn_part) + out_bias[0]
     resid_own = source_own + attn_own
     hat_two, inv_two = normalize(resid_own)
     normed_rows = (hat_two * norm_gain[1] + norm_bias[1]).astype(jnp.bfloat16)
@@ -118,7 +125,7 @@
     hidden = jnp.dot(normed_two, w_up, preferred_element_type=jnp.float32) + up_bias
     active = jax.nn.gelu(hidden, approximate=False).astype(jnp.bfloat16)
     mlp_part = jnp.dot(active, w_down, preferred_element_type=jnp.float32)
-    branch_own = lax.psum_scatter(mlp_part, "tensor", scatter_dimension=0, tiled=True) + out_bias[1]
+    branch_own = scatter_rows(mlp_part) + out_bias[1]
     output = (resid_own + branch_own).astype(jnp.bfloat16)
     stat_terms = jnp.stack(
         [
@@ -140,7 +147,7 @@
     grad_up_bias = jnp.sum(grad_hidden.astype(jnp.float32), axis=0)
     grad_up = jnp.einsum("rd,rf->df", normed_two, grad_hidden, preferred_element_type=jnp.float32)
     norm_part = jnp.einsum("rf,df->rd", grad_hidden, w_up, preferred_element_type=jnp.float32)
-    grad_norm_own = lax.psum_scatter(norm_part, "tensor", scatter_dimension=0, tiled=True)
+    grad_norm_own = scatter_rows(norm_part)
     grad_resid_own = own_rows(grad_full) + norm_back(grad_norm_own, hat_two, inv_two, norm_gain[1])
     grad_attn = lax.all_gather(grad_resid_own.astype(jnp.bfloat16), "tensor", axis=0, tiled=True)
     gain_two = jnp.sum(grad_norm_own * hat_two, axis=0)
@@ -182,7 +189,7 @@
     )
     grad_qkv = jnp.einsum("rd,tre->tde", normed_one, grad_proj, preferred_element_type=jnp.float32)
     input_part = jnp.einsum("tre,tde->rd", grad_proj, w_qkv, preferred_element_type=jnp.float32)
-    grad_in_own = lax.psum_scatter(input_part, "tensor", scatter_dimension=0, tiled=True)
+    grad_in_own = scatter_rows(input_part)
     hat_one_own = own_rows(hat_one)
     grad_tokens = grad_resid_own + norm_back(
         grad_in_own, hat_one_own, own_rows(inv_one), norm_gain[0]
@@ -195,9 +202,14 @@
     gain_sums, shift_sums, bias_sums = lax.psum(
         (gain_terms, shift_terms, bias_terms), ("dp", "tensor")
     )
-    grad_qkv, grad_qv, grad_table, grad_wout, grad_up, grad_up_bias, grad_down = lax.psum(
-        (grad_qkv, grad_qv, grad_table, grad_wout, grad_up, grad_up_bias, grad_down), "dp"
-    )
+    grad_qv, grad_table, grad_up_bias = lax.psum((grad_qv, grad_table, grad_up_bias), "dp")
+    grad_qkv, grad_wout, grad_up, grad_down = [
+        total.astype(jnp.float32)
+        for total in lax.psum(
+            [part.astype(jnp.bfloat16) for part in (grad_qkv, grad_wout, grad_up, grad_down)],
+            "dp",
+        )
+    ]
     live_count = jnp.maximum(stat_total[3], 1.0) * tokens.shape[1]
     root_means = jnp.sqrt(stat_total[0:3] / live_count)
     return (

time: 673 us -> 485 us (0.72)
  waiting for transfers between devices: 413 us -> 237 us
  local copies, waits for them, and re-layouts: 60.4 us -> 49.3 us
    reduce_scatter x4, waiting for transfers between devices: 239 us -> 129 us  [scatter_rows(): lax.psum_scatter(part.astype(jnp.bfloat16), 'tensor', scatter_dimension=0...]
    psum x1, waiting for transfers between devices: 109 us -> 42.5 us  [on_device(): lax.psum([part.astype(jnp.bfloat16) for part in (grad_qkv, grad_wout, gra...]
    unnamed x110 -> x109, local copies, waits for them, and re-layouts: 16.8 us -> 5.64 us
    convert_element_type x0 -> x4, other arithmetic: none -> 9.88 us  [the longest x3 6.04 us: on_device(): total.astype(jnp.float32)]
  transfers between devices with their start and end apart: 7 -> 7, of which waited for: 7 -> 7; matrix products, arithmetic and copies ran while one was open for 9% -> 14% of each run, Pallas kernels for 0% -> 0%
where the time goes in v1:
time: 485 us; the launch traced here: 476 us
  waiting for transfers between devices  237 us (49%)
  matrix products  73 us (15%)
  blocking collectives  65.1 us (13%)
  local copies, waits for them, and re-layouts  49.3 us (10%)
  other arithmetic  34.9 us (7%)
  between operations  15.8 us (3%)
    reduce_scatter x4, waiting for transfers between devices, scatter_rows(): lax.psum_scatter(part.astype(jnp.bfloat16), 'tensor', scatter_dimension=0...  129 us
    psum x1, waiting for transfers between devices, on_device(): lax.psum([part.astype(jnp.bfloat16) for part in (grad_qkv, grad_wout, gra...  42.5 us
    psum x1, blocking collectives, on_device(): lax.psum((gain_terms, shift_terms, bias_terms), ('dp', 'tensor'))  39.7 us
    all_gather x1, waiting for transfers between devices, on_device(): normed_two = lax.all_gather(normed_rows, 'tensor', axis=0, tiled=True)  37.1 us
    all_gather x1, waiting for transfers between devices, on_device(): lax.all_gather(grad_resid_own.astype(jnp.bfloat16), 'tensor', axis=0, til...  27.9 us
    psum x1, blocking collectives, on_device(): lax.psum((grad_qv, grad_table, grad_up_bias), 'dp')  25.4 us
    reshape x2, local copies, waits for them, and re-layouts, relative_back(): gradient.reshape(heads_count, window_side, window_side, window_side, wind...  16.3 us
    dot_general x1, matrix products, on_device(): jnp.dot(normed_two, w_up, preferred_element_type=jnp.float32) + up_bias  10.8 us
  transfers between devices with their start and end apart: 7, of which 7 were waited for; matrix products, arithmetic and copies ran while one was open for 14% of the time, Pallas kernels for 0%

profile of v1, /device:TPU:0, one launch (start us, length us, event | category | flops | bytes accessed | tf_op | source)
XLA Modules:
  0.0 476.1 jit_solution(3866228508899291969)
XLA Ops:
  8.7 4.8 %convolution_bitcast_fusion = f32[8,10,10,10,10]{4,3,2,1,0:T(8,128)} fusion(f32[8,19,10,10,1]{1,3,4,2,0:T(8,128)S(1)} %convolution_bitcast_fusion.2, s32[10,10]{1,0:T(8,128)S(1)} %subtract_add_fusion), kind=kOutput, calls=%fused_computation.39 | convolution fusion | flops 18241900 | bytes 381200 | tf_op jit(solution)/shard_map/ija,klb,hab->hikjl/dot_general | solution.py:42
  13.5 4.4 reshape.173
  32.4 2.4 squeeze.12
  39.6 3.0 convolution_convert_fusion.2
  43.1 3.5 convert_element_type.123
  46.7 35.3 %reduce-scatter.5.cloned.1.call-done = bf16[200,1024]{1,0:T(8,128)(2,1)} async-done(((bf16[800,1024]{1,0:T(8,128)(2,1)}), bf16[200,1024]{1,0:T(8,128)(2,1)}) %reduce-scatter.5.cloned.1.call-update) | async-done | bytes 409616 | tf_op jit(solution)/shard_map/reduce_scatter | solution.py:55
  84.7 37.1 %all-gather.3.cloned.1.call-done = bf16[800,1024]{1,0:T(8,128)(2,1)} async-done(((bf16[200,1024]{1,0:T(8,128)(2,1)}), bf16[800,1024]{1,0:T(8,128)(2,1)}) %all-gather.3.cloned.1.call-update) | async-done | bytes 1638416 | tf_op jit(solution)/shard_map/all_gather | solution.py:124
  121.8 10.8 %fusion.2 = (bf16[800,1024]{1,0:T(8,128)(2,1)}, f32[800,1024]{1,0:T(8,128)S(1)}) fusion(f32[1024]{0:T(1024)S(1)} %copy-done.50, bf16[800,1024]{1,0:T(8,128)(2,1)} %all-gather.3.cloned.1.call-done, bf16[1024,1024]{1,0:T(8,128)(2,1)S(1)} %copy-done), kind=kOutput, calls=%fused_computation.11 | convolution fusion | flops 1731788800 | bytes 8654848 | tf_op jit(solution)/shard_map/dot_general | solution.py:125
  132.7 3.7 convert_reduce_fusion.1
  137.6 3.1 convolution_convert_fusion.3
  140.7 5.3 %convolution_convert_fusion.4 = bf16[800,1024]{1,0:T(8,128)(2,1)} fusion(bf16[800,1024]{1,0:T(8,128)(2,1)} %get-tuple-element.100, bf16[1024,1024]{1,0:T(8,128)(2,1)} %param.24), kind=kOutput, calls=%fused_computation.47 | convolution fusion | flops 1678540800 | bytes 5373952 | tf_op jit(solution)/shard_map/dot_general | solution.py:127
  146.9 29.1 %reduce-scatter.9.cloned.1.call-done = bf16[200,1024]{1,0:T(8,128)(2,1)} async-done(((bf16[800,1024]{1,0:T(8,128)(2,1)}), bf16[200,1024]{1,0:T(8,128)(2,1)}) %reduce-scatter.9.cloned.1.call-update) | async-done | bytes 409616 | tf_op jit(solution)/shard_map/reduce_scatter | solution.py:55
  178.1 35.5 %reduce-scatter.7.cloned.1.call-done = bf16[200,1024]{1,0:T(8,128)(2,1)} async-done(((bf16[800,1024]{1,0:T(8,128)(2,1)}), bf16[200,1024]{1,0:T(8,128)(2,1)}) %reduce-scatter.7.cloned.1.call-update) | async-done | bytes 409616 | tf_op jit(solution)/shard_map/reduce_scatter | solution.py:55
  213.6 3.8 fusion.81
  217.8 5.3 %convolution_convert_fusion = bf16[1024,1024]{1,0:T(8,128)(2,1)} fusion(bf16[800,1024]{1,0:T(8,128)(2,1)} %get-tuple-element.100, bf16[800,1024]{1,0:T(8,128)(2,1)S(1)} %copy-done.26), kind=kOutput, calls=%fused_computation.43 | convolution fusion | flops 1678770176 | bytes 5373952 | tf_op jit(solution)/shard_map/rf,rd->fd/dot_general | solution.py:140
  223.1 3.7 convolution_convert_fusion.1
  226.8 27.9 %all-gather.5.cloned.1.call-done = bf16[800,1024]{1,0:T(8,128)(2,1)} async-done(((bf16[200,1024]{1,0:T(8,128)(2,1)}), bf16[800,1024]{1,0:T(8,128)(2,1)}) %all-gather.5.cloned.1.call-update) | async-done | bytes 1638416 | tf_op jit(solution)/shard_map/all_gather | solution.py:152
  254.7 2.9 convolution_convert_fusion.7
  262.0 2.8 convert_reduce_fusion.5
  274.9 4.4 fusion.23
  281.8 4.1 bitcast_convert_fusion
  288.1 2.6 pad_maximum_fusion.8
  290.9 4.0 reshape.174
  294.9 12.4 %copy.101 = f32[8,10,10,10,10]{4,3,1,2,0:T(8,128)} copy(f32[8,10,10,10,10]{2,1,4,3,0:T(8,128)} %reshape.174) | data formatting | bytes 640000 | tf_op jit(solution)/shard_map/reshape | solution.py:49
  307.2 8.3 %convolution_bitcast_fusion.1 = f32[19,8,10,10]{0,3,2,1:T(8,128)S(1)} fusion(f32[8,10,10,10,10]{4,3,1,2,0:T(8,128)} %copy.101, s32[10,10]{1,0:T(8,128)S(1)} %copy-done.24), kind=kOutput, calls=%fused_computation.62 | convolution fusion | flops 18241900 | bytes 381200 | tf_op jit(solution)/shard_map/hikjl,ija,klb->hab/dot_general | solution.py:50
  316.3 25.4 %all-reduce.1 = (f32[2,256]{1,0:T(2,128)}, f32[8,361]{1,0:T(8,128)}, f32[1024]{0:T(1024)}) all-reduce(f32[2,256]{1,0:T(2,128)S(1)} %pad_maximum_fusion.7, f32[8,361]{1,0:T(8,128)S(1)} %reshape.160, f32[1024]{0:T(1024)S(1)} %copy-done.45), channel_id=1, replica_groups=mesh['dp'=8,'tensor'=4] {'dp'}, use_global_device_ids=true, to_apply=%region_24.0 | all-reduce | flops 4424 | bytes 35392 | tf_op jit(solution)/shard_map/psum | solution.py:205
  341.7 42.5 %all-reduce.5.cloned.1.call-done = (bf16[3,1024,256]{1,2,0:T(8,128)(2,1)}, bf16[256,1024]{1,0:T(8,128)(2,1)}, bf16[1024,1024]{1,0:T(8,128)(2,1)}, bf16[1024,1024]{1,0:T(8,128)(2,1)}) async-done(((bf16[3,1024,256]{1,2,0:T(8,128)(2,1)}, bf16[256,1024]{1,0:T(8,128)(2,1)}, bf16[1024,1024]{1,0:T(8,128)(2,1)}, bf16[1024,1024]{1,0:T(8,128)(2,1)}), (bf16[3,1024,256]{1,2,0:T(8,128)(2,1)}, ...) | async-done | bytes 6291472 | tf_op jit(solution)/shard_map/psum | solution.py:208
  384.2 3.2 copy.93
  388.5 2.5 convert_element_type.157
  391.0 2.5 convert_element_type.160
  393.5 29.6 %reduce-scatter.11.cloned.1.call-done = bf16[200,1024]{1,0:T(8,128)(2,1)} async-done(((bf16[800,1024]{1,0:T(8,128)(2,1)}), bf16[200,1024]{1,0:T(8,128)(2,1)}) %reduce-scatter.11.cloned.1.call-update) | async-done | bytes 409616 | tf_op jit(solution)/shard_map/reduce_scatter | solution.py:55
  424.9 39.7 %all-reduce = (f32[2,1024]{1,0:T(2,128)}, f32[2,1024]{1,0:T(2,128)}, f32[2,1024]{1,0:T(2,128)}, f32[4]{0:T(128)S(1)}) all-reduce(f32[2,1024]{1,0:T(2,128)S(1)} %pad_maximum_fusion.3, f32[2,1024]{1,0:T(2,128)S(1)} %pad_maximum_fusion.4, f32[2,1024]{1,0:T(2,128)S(1)} %pad_maximum_fusion.5, ...), channel_id=1, replica_groups=mesh['dp'=8,'tensor'=4] {'dp','tensor'}, use_global_device_ids=true, to_apply=%region_17.0 | all-reduce | flops 6148 | bytes 49184 | tf_op jit(solution)/shard_map/psum | solution.py:202
  (194 shorter events, 54.7 us)
Async XLA Ops:
  7.2 114.6 %copy-start = (bf16[1024,1024]{1,0:T(8,128)(2,1)S(1)}, bf16[1024,1024]{1,0:T(8,128)(2,1)}, u32[]{:S(2)}) copy-start(bf16[1024,1024]{1,0:T(8,128)(2,1)} %param.22) | copy-start | bytes 6291460
  7.2 74.7 %reduce-scatter.5.cloned.1.call-start = ((), (), s32[]{:S(2)}) async-start(), calls=%async_computation.4 | async-start | bytes 2048000 | tf_op jit(solution)/shard_map/reduce_scatter | solution.py:55
  13.5 5.4 %copy-start.46 = (f32[2,256]{1,0:T(2,128)S(1)}, f32[2,256]{1,0:T(2,128)}, u32[]{:S(2)}) copy-start(f32[2,256]{1,0:T(2,128)} %param.18) | copy-start | bytes 6148
  13.5 5.4 %copy-start.41 = (f32[2,1024]{1,0:T(2,128)S(1)}, f32[2,1024]{1,0:T(2,128)}, u32[]{:S(2)}) copy-start(f32[2,1024]{1,0:T(2,128)} %param.16) | copy-start | bytes 24580
  13.5 6.0 %copy-start.42 = (f32[2,1024]{1,0:T(2,128)S(1)}, f32[2,1024]{1,0:T(2,128)}, u32[]{:S(2)}) copy-start(f32[2,1024]{1,0:T(2,128)} %param.15) | copy-start | bytes 24580
  20.1 5.7 %copy-start.31 = (f32[1,1024]{1,0:T(1,128)}, f32[1,1024]{1,0:T(1,128)S(1)}, u32[]{:S(2)}) copy-start(f32[1,1024]{1,0:T(1,128)S(1)} %get-tuple-element.93) | copy-start | bytes 12292
  27.6 9.4 %copy-start.6 = (bf16[8,100,8,32]{1,0,3,2:T(8,128)(2,1)}, bf16[8,100,8,32]{1,0,3,2:T(8,128)(2,1)S(1)}, u32[]{:S(2)}) copy-start(bf16[8,100,8,32]{1,0,3,2:T(8,128)(2,1)S(1)} %squeeze.14) | copy-start | bytes 1228804
  31.4 5.6 %copy-start.8 = (bf16[8,100,8,32]{1,0,3,2:T(8,128)(2,1)}, bf16[8,100,8,32]{1,0,3,2:T(8,128)(2,1)S(1)}, u32[]{:S(2)}) copy-start(bf16[8,100,8,32]{1,0,3,2:T(8,128)(2,1)S(1)} %squeeze.13) | copy-start | bytes 1228804
  39.5 7.1 %copy-start.16 = (bf16[800,256]{0,1:T(8,128)(2,1)}, bf16[800,256]{0,1:T(8,128)(2,1)S(1)}, u32[]{:S(2)}) copy-start(bf16[800,256]{0,1:T(8,128)(2,1)S(1)} %reshape.157) | copy-start | bytes 1228804
  42.6 41.1 %copy-start.28 = (f32[1,1024]{1,0:T(1,128)S(1)}, f32[1,1024]{1,0:T(1,128)}, u32[]{:S(2)}) copy-start(f32[1,1024]{1,0:T(1,128)} %get-tuple-element.92) | copy-start | bytes 12292
  42.6 41.1 %copy-start.39 = (f32[1,1024]{1,0:T(1,128)S(1)}, f32[1,1024]{1,0:T(1,128)}, u32[]{:S(2)}) copy-start(f32[1,1024]{1,0:T(1,128)} %get-tuple-element.94) | copy-start | bytes 12292
  42.6 79.2 %all-gather.3.cloned.1.call-start = ((), (), s32[]{:S(2)}) async-start(), calls=%async_computation.5 | async-start | bytes 2048000 | tf_op jit(solution)/shard_map/all_gather | solution.py:124
  46.6 75.2 %copy-start.50 = (f32[1024]{0:T(1024)S(1)}, f32[1024]{0:T(1024)}, u32[]{:S(2)}) copy-start(f32[1024]{0:T(1024)} %param.23) | copy-start | bytes 12292
  84.6 91.4 %reduce-scatter.9.cloned.1.call-start = ((), (), s32[]{:S(2)}) async-start(), calls=%async_computation.7 | async-start | bytes 2048000 | tf_op jit(solution)/shard_map/reduce_scatter | solution.py:55
  121.8 10.8 %copy-start.25 = (bf16[800,1024]{1,0:T(8,128)(2,1)S(1)}, bf16[800,1024]{1,0:T(8,128)(2,1)}, u32[]{:S(2)}) copy-start(bf16[800,1024]{1,0:T(8,128)(2,1)} %param.25) | copy-start | bytes 4915204
  121.8 10.8 %copy-start.47 = (bf16[1024,1024]{1,0:T(8,128)(2,1)S(1)}, bf16[1024,1024]{1,0:T(8,128)(2,1)}, u32[]{:S(2)}) copy-start(bf16[1024,1024]{1,0:T(8,128)(2,1)} %param.24) | copy-start | bytes 6291460
  140.6 73.0 %reduce-scatter.7.cloned.1.call-start = ((), (), s32[]{:S(2)}) async-start(), calls=%async_computation.6 | async-start | bytes 2048000 | tf_op jit(solution)/shard_map/reduce_scatter | solution.py:55
  140.7 5.4 %copy-start.51 = (s32[8]{0:T(128)S(1)}, s32[8]{0:T(128)}, u32[]{:S(2)}) copy-start(s32[8]{0:T(128)} %param.14) | copy-start | bytes 100
  140.7 72.9 %copy-start.19 = (bf16[200,1024]{1,0:T(8,128)(2,1)S(1)}, bf16[200,1024]{1,0:T(8,128)(2,1)}, u32[]{:S(2)}) copy-start(bf16[200,1024]{1,0:T(8,128)(2,1)} %reduce-scatter.5.cloned.1.call-done) | copy-start | bytes 1228804
  140.7 72.9 %copy-start.26 = (bf16[800,1024]{1,0:T(8,128)(2,1)S(1)}, bf16[800,1024]{1,0:T(8,128)(2,1)}, u32[]{:S(2)}) copy-start(bf16[800,1024]{1,0:T(8,128)(2,1)} %param.25) | copy-start | bytes 4915204
  146.0 108.6 %all-gather.5.cloned.1.call-start = ((), (), s32[]{:S(2)}) async-start(), calls=%async_computation.8 | async-start | bytes 2048000 | tf_op jit(solution)/shard_map/all_gather | solution.py:152
  217.5 166.7 %all-reduce.5.cloned.1.call-start = ((), (), s32[]{:S(2)}) async-start(), calls=%async_computation.10 | async-start | bytes 12582912 | tf_op jit(solution)/shard_map/psum | solution.py:208
  226.8 35.2 %copy-start.3 = (f32[8,8,100,100]{2,3,1,0:T(8,128)S(1)}, f32[8,8,100,100]{2,3,1,0:T(8,128)}, u32[]{:S(2)}) copy-start(f32[8,8,100,100]{2,3,1,0:T(8,128)} %copy-done.2) | copy-start | bytes 7680004
  280.9 142.2 %reduce-scatter.11.cloned.1.call-start = ((), (), s32[]{:S(2)}) async-start(), calls=%async_computation.9 | async-start | bytes 2048000 | tf_op jit(solution)/shard_map/reduce_scatter | solution.py:55
  294.9 12.4 %copy-start.24 = (s32[10,10]{1,0:T(8,128)S(1)}, s32[10,10]{1,0:T(8,128)}, u32[]{:S(2)}) copy-start(s32[10,10]{1,0:T(8,128)} %copy-done.23) | copy-start | bytes 1204
  307.2 9.1 %copy-start.45 = (f32[1024]{0:T(1024)S(1)}, f32[1024]{0:T(1024)}, u32[]{:S(2)}) copy-start(f32[1024]{0:T(1024)} %get-tuple-element.108) | copy-start | bytes 12292
  391.0 32.1 %copy-start.32 = (f32[1,1024]{1,0:T(1,128)S(1)}, f32[1,1024]{1,0:T(1,128)}, u32[]{:S(2)}) copy-start(f32[1,1024]{1,0:T(1,128)} %copy-done.31) | copy-start | bytes 12292
  391.0 33.9 %copy-start.38 = (f32[1024]{0:T(1024)S(1)}, f32[1024]{0:T(1024)}, u32[]{:S(2)}) copy-start(f32[1024]{0:T(1024)} %get-tuple-element.54) | copy-start | bytes 12292
  391.0 33.9 %copy-start.37 = (f32[1024]{0:T(1024)S(1)}, f32[1024]{0:T(1024)}, u32[]{:S(2)}) copy-start(f32[1024]{0:T(1024)} %get-tuple-element.59) | copy-start | bytes 12292
  391.0 33.9 %copy-start.40 = (f32[1024]{0:T(1024)S(1)}, f32[1024]{0:T(1024)}, u32[]{:S(2)}) copy-start(f32[1024]{0:T(1024)} %get-tuple-element.82) | copy-start | bytes 12292
  391.0 75.4 %copy-start.11 = (f32[200,1024]{1,0:T(8,128)S(1)}, f32[200,1024]{1,0:T(8,128)}, u32[]{:S(2)}) copy-start(f32[200,1024]{1,0:T(8,128)} %get-tuple-element.79) | copy-start | bytes 2457604
  391.0 77.8 %copy-start.1 = (bf16[1024,1024]{1,0:T(8,128)(2,1)S(1)}, bf16[1024,1024]{1,0:T(8,128)(2,1)}, u32[]{:S(2)}) copy-start(bf16[1024,1024]{1,0:T(8,128)(2,1)} %param.22) | copy-start | bytes 6291460
  (29 other events, 104.7 us)
Sparse Core Ops, SparseCore 0:
  42.7 39.1 reduce-scatter.4
  84.8 36.9 all-gather.2
  140.8 35.2 reduce-scatter.8
  178.2 35.3 reduce-scatter.6
  217.6 36.9 all-gather.4
  281.0 103.1 all-reduce.4
  386.5 36.5 reduce-scatter.10
